TPU v7x, 256 devices: a whole 4x4x8 slice. The times are simulated.
256 devices in a mesh: row: 8 (over x, z_hi), col: 32 (over y, z_lo, core).
Axes of the slice: x: 4, y: 4, z: 8 (z_hi: 2, z_lo: 4; z = z_hi * 4 + z_lo), core: 2. Of those that a mesh axis runs over, the one named last changes fastest.
Arguments:
- symmetric: float32 [12288, 12288], P('row', 'col'), may hold values from -24 to 24, as said below
Outputs:
- reduced: float32 [12288, 12288], P('row', 'col')
Inputs may be any that keep to these rules, and one draw needn't show every extreme that they name: symmetric equals its transpose.
All inputs are finite; a program needn't handle non-finite values.
Results may differ from a plain program's by a relative error of at most 0.0001.
Values sent between devices are 32-bit elements; how exact they have to be, the bound alone decides.
No kernel may reach another device: no remote copies, remote signals or barrier semaphores. Data moves between devices by JAX's collectives and lax.ppermute only.
A program may use at most 64 MiB of HBM per device.

v0:
```python
import math
import jax
import jax.numpy as jnp
from jax import lax
from jax.sharding import Mesh
from jax.sharding import PartitionSpec as P

N = 12288
B = 256
ROW = ("row_0", "row_1")
COL = ("col_0", "col_1", "col_2")
HIGH = lax.Precision.HIGHEST


def padded_to(lines, size):
    spare = -len(lines) % size
    return jnp.pad(lines, [(0, spare)] + [(0, 0)] * (lines.ndim - 1))


def broadcast_by_parts(shard, axis, root):
    lines = jnp.where(lax.axis_index(axis) == root, shard, jnp.zeros_like(shard)).reshape(
        -1, *shard.shape[1:][-1:]
    )
    padded = padded_to(lines, lax.axis_size(axis))
    own = lax.psum_scatter(padded, axis, scatter_dimension=0, tiled=True)
    return lax.all_gather(own, axis, axis=0, tiled=True)[: len(lines)].reshape(shard.shape)


def broadcast_by_axis(shard, axes, root):
    shard = jnp.where(lax.axis_index(axes) == root, shard, jnp.zeros_like(shard))
    for axis in axes:
        shard = lax.psum(shard, axis)
    return shard


def in_blocks(shard, dim, size):
    dims = shard.shape
    parts = shard.reshape(*dims[:dim], size, dims[dim] // size, *dims[dim + 1 :])
    return jnp.moveaxis(parts, dim, 0)


def summed_on_arrival(shard, axis, dim):
    size = lax.axis_size(axis)
    parts = lax.all_to_all(in_blocks(shard, dim, size), axis, 0, 0, tiled=True)
    return jnp.sum(parts, axis=0)


def sum_in_two_steps(shard, axes, dim):
    far, near = axes
    own = summed_on_arrival(in_blocks(shard, dim, lax.axis_size(far)), near, dim + 1)
    return jnp.sum(lax.all_to_all(own, far, 0, 0, tiled=True), axis=0)


def from_everyone(shard, axis):
    size = lax.axis_size(axis)
    return lax.all_to_all(
        jnp.broadcast_to(shard[None], (size, *shard.shape)), axis, 0, 0, tiled=True
    )


def in_order(parts, dim):
    parts = jnp.moveaxis(parts, 0, dim)
    dims = parts.shape
    return parts.reshape(*dims[:dim], dims[dim] * dims[dim + 1], *dims[dim + 2 :])


def gather_axes(shard, axes, dim):
    far, near = axes
    parts = from_everyone(from_everyone(shard, far), near)
    return in_order(parts.swapaxes(0, 1).reshape(-1, *shard.shape), dim)


def total_of(shard, axes):
    lines = shard.reshape(-1, shard.shape[-1])
    own = sum_in_two_steps(
        padded_to(lines, lax.axis_size(axes[0]) * lax.axis_size(axes[1])), axes, 0
    )
    whole = gather_axes(own, axes, 0)
    return whole[: len(lines)].reshape(shard.shape)


def over_copies(shard, axis):
    return from_everyone(shard, axis).sum(axis=0)


def broadcast(shard, axis, root):
    return lax.dynamic_index_in_dim(lax.all_gather(shard, axis), root, 0, keepdims=False)


def contract(left_op, right_op, left_dim, right_dim):
    return lax.dot_general(
        left_op,
        right_op,
        (((left_dim,), (right_dim,)), ((), ())),
        precision=HIGH,
        preferred_element_type=jnp.float32,
    )


def per_device(symmetric):
    current = symmetric
    rows_dev, cols_dev = current.shape
    row_count_axis = lax.axis_size(ROW)
    col_count_axis = lax.axis_size(COL)
    row_at = lax.axis_index(ROW)
    col_at = lax.axis_index(COL)
    per_row = col_count_axis // row_count_axis
    global_rows = row_at * rows_dev + jnp.arange(rows_dev, dtype=jnp.int32)
    global_cols = col_at * cols_dev + jnp.arange(cols_dev, dtype=jnp.int32)
    band_index = jnp.arange(B, dtype=jnp.int32)
    identity = jnp.eye(B, dtype=jnp.float32)
    which = 0
    first_col = which * B
    below = first_col + B
    column_strip = broadcast_by_parts(current[:, first_col : first_col + B], COL, 0)
    panel_cols = jnp.where((global_rows >= below)[:, None], column_strip, jnp.float32(0.0))
    row_strip = broadcast_by_axis(current[first_col : first_col + B, :], ROW, 0)
    panel_trans = jnp.where((global_cols >= below)[None, :], row_strip, jnp.float32(0.0))
    gram_part = contract(panel_cols, panel_cols, 0, 0)
    leading_part = jnp.where(row_at == 0, panel_cols[below : below + B], jnp.float32(0.0))
    gram, leading_rows = lax.psum((gram_part, leading_part), ROW)
    lower_factor = jnp.linalg.cholesky(gram)
    basis_rows = lax.linalg.triangular_solve(
        lower_factor, panel_cols, left_side=False, lower=True, transpose_a=True
    )
    leading = lax.linalg.triangular_solve(
        lower_factor, leading_rows, left_side=False, lower=True, transpose_a=True
    )
    row_unit = (global_rows[:, None] - below == band_index[None, :]).astype(jnp.float32)
    reflector = basis_rows - row_unit
    col_unit = (band_index[:, None] == global_cols[None, :] - below).astype(jnp.float32)
    reflector_t = (
        lax.linalg.triangular_solve(lower_factor, panel_trans, left_side=True, lower=True)
        - col_unit
    )
    shifted = identity - leading
    normal_mat = contract(shifted, shifted, 0, 0)
    normal_chol = jnp.linalg.cholesky(normal_mat)
    interim = lax.linalg.triangular_solve(normal_chol, shifted.T, left_side=True, lower=True)
    t_mat = lax.linalg.triangular_solve(
        normal_chol, interim, left_side=True, lower=True, transpose_a=True
    )
    u_row = total_of(contract(current, reflector_t, 1, 1), (("col_0", "col_1"), "col_2"))
    core_sum = over_copies(contract(reflector, u_row, 0, 0), ROW)
    middle = contract(contract(t_mat, core_sum, 1, 0), t_mat, 1, 1)
    w_row = contract(u_row, t_mat, 1, 1) - 0.5 * contract(reflector, middle, 1, 0)
    offset = col_at % per_row * cols_dev
    w_piece = lax.dynamic_slice_in_dim(w_row, offset, cols_dev, 0)
    w_col = broadcast(w_piece, ROW, col_at // per_row)
    first_term = contract(reflector, w_col, 1, 1)
    second_term = contract(w_row, reflector_t, 1, 0)
    current = current - first_term - second_term
    factors = [lower_factor]
    inverse_root = jnp.float32(1.0 / math.sqrt(N))
    which = 0
    first_col = which * B
    below = first_col + B
    r_mat = factors[which].T * inverse_root
    old_strip = current[:, first_col : first_col + B]
    placed = jnp.zeros((rows_dev, B), jnp.float32).at[below : below + B].set(r_mat)
    inside = global_rows[:, None] < below + B
    updated = jnp.where(
        global_rows[:, None] >= below, jnp.where(inside, placed, jnp.float32(0.0)), old_strip
    )
    updated = jnp.where(col_at == 0, updated, old_strip)
    current = current.at[:, first_col : first_col + B].set(updated)
    old_top = current[first_col : first_col + B, :]
    onehot = (global_cols[:, None] - below == band_index[None, :]).astype(jnp.float32)
    mirror = contract(r_mat, onehot, 0, 1)
    new_top = jnp.where((global_cols >= below)[None, :], mirror, old_top)
    new_top = jnp.where(row_at == 0, new_top, old_top)
    current = current.at[first_col : first_col + B, :].set(new_top)
    return current


def solution(mesh):
    split = Mesh(mesh.devices.reshape(4, 2, 4, 4, 2), ("row_0", "row_1", "col_0", "col_1", "col_2"))
    return jax.shard_map(
        per_device, mesh=split, in_specs=(P(ROW, COL),), out_specs=P(ROW, COL), check_vma=False
    )
```

profile of v0, /device:TPU:1, one launch (start us, length us, event | category | flops | bytes accessed | tf_op | source)
XLA Modules:
  0.0 691.2 jit_solution(5647719800519934500)
XLA Ops:
  7.4 2.0 copy.58
  9.4 1.3 slice_select_fusion
  10.8 3.0 copy.70
  14.8 145.9 %reduce-scatter.4.cloned.1.call-done = f32[48,256]{1,0:T(8,128)} async-done(((f32[1536,256]{1,0:T(8,128)}), f32[48,256]{1,0:T(8,128)}) %reduce-scatter.4.cloned.1.call-update) | async-done | bytes 49168 | tf_op jit(solution)/shard_map/reduce_scatter | solution.py:25
  161.3 74.1 %all-gather.4.cloned.1.call-done = f32[1536,256]{1,0:T(8,128)} async-done(((f32[48,256]{1,0:T(8,128)}), f32[1536,256]{1,0:T(8,128)}) %all-gather.4.cloned.1.call-update) | async-done | bytes 1572880 | tf_op jit(solution)/shard_map/all_gather | solution.py:26
  235.4 1.9 copy.46
  238.1 2.1 fusion.67
  240.4 1.1 broadcast_select_fusion.1
  241.5 105.0 %all-reduce.11.cloned.1.call-done = (f32[256,256]{0,1:T(8,128)}, f32[256,256]{0,1:T(8,128)}) async-done(((f32[256,256]{0,1:T(8,128)}, f32[256,256]{0,1:T(8,128)}), (f32[256,256]{0,1:T(8,128)}, f32[256,256]{0,1:T(8,128)})) %all-reduce.11.cloned.1.call-update) | async-done | bytes 524304 | tf_op jit(solution)/shard_map/psum | solution.py:121
  346.5 1.1 copy.48
  347.6 1.0 fusion.10
  348.6 11.7 %cholesky.130 = f32[128,128]{1,0:T(8,128)S(1)} custom-call(f32[128,128]{1,0:T(8,128)S(1)} %cholesky.194), custom_call_target="Cholesky" | custom-call | tf_op jit(solution)/shard_map/jit(cholesky)/cholesky | solution.py:122
  360.4 9.8 %custom-call.23 = f32[1,128,128]{1,2,0:T(8,128)S(1)} custom-call(f32[1,128,128]{2,1,0:T(8,128)S(1)} %get-tuple-element.89), custom_call_target="InvertDiagBlocksLowerTriangular" | custom-call | tf_op jit(solution)/shard_map/jit(cholesky)/cholesky | solution.py:122
  370.7 11.9 %cholesky.147 = f32[128,128]{1,0:T(8,128)S(1)} custom-call(f32[128,128]{1,0:T(8,128)S(1)} %convolution_subtract_fusion.8), custom_call_target="Cholesky" | custom-call | tf_op jit(solution)/shard_map/jit(cholesky)/cholesky | solution.py:122
  385.3 4.0 while.5
  385.9 1.4 bitcast_dynamic-update-slice_fusion.4
  387.9 1.4 bitcast_dynamic-update-slice_fusion.4
  389.3 19.7 %custom-call.20 = f32[2,128,128]{1,2,0:T(8,128)S(1)} custom-call(f32[2,128,128]{2,1,0:T(8,128)S(1)} %get-tuple-element.49), custom_call_target="InvertDiagBlocksLowerTriangular" | custom-call | tf_op jit(solution)/shard_map/triangular_solve | solution.py:123
  411.0 5.5 convolution_bitcast_fusion
  416.6 1.9 copy.52
  418.6 12.3 %all_to_all.25 = f32[2,16,48,256]{3,2,1,0:T(8,128)S(1)} all-to-all(f32[2,16,48,256]{3,2,1,0:T(8,128)S(1)} %copy.53), channel_id=1, replica_groups=mesh['row_0'=4,'row_1'=2,'col_0'=4,'col_1'=4,'col_2'=2] {'col_2'}, dimensions={0} | all-to-all | bytes 3145728 | tf_op jit(solution)/shard_map/all_to_all | solution.py:44
  430.9 1.0 reduce_sum.27
  431.9 4.5 all-to-all-start.1
  436.8 21.0 %all-to-all-done.1 = f32[16,48,256]{2,1,0:T(8,128)S(1)} async-done(((f32[16,48,256]{2,1,0:T(8,128)}), f32[16,48,256]{2,1,0:T(8,128)S(1)}, u32[]{:S(2)}, u32[]{:S(2)}) %all-to-all-start.1) | async-done | bytes 786464 | tf_op jit(solution)/shard_map/all_to_all | solution.py:51
  457.9 1.0 broadcast_in_dim.49
  458.9 4.5 all-to-all-start.2
  463.5 1.2 convolution_subtract_fusion.6
  466.3 11.7 %cholesky.164 = f32[128,128]{1,0:T(8,128)S(1)} custom-call(f32[128,128]{1,0:T(8,128)S(1)} %cholesky.197), custom_call_target="Cholesky" | custom-call | tf_op jit(solution)/shard_map/jit(cholesky)/cholesky | solution.py:138
  478.0 0.9 fusion.4
  478.9 0.8 convolution_subtract_fusion.2
  479.8 0.8 fusion.44
  480.6 4.2 all-to-all-done.2
  484.8 1.3 broadcast_in_dim.50
  486.2 6.3 all_to_all.26
  492.6 1.6 fusion.6
  494.3 1.5 broadcast_in_dim.51
  495.8 4.3 all-to-all-start.4
  500.4 1.2 select_reduce_fusion.1
  502.4 10.6 %custom-call.24 = f32[1,128,128]{1,2,0:T(8,128)S(1)} custom-call(f32[1,128,128]{2,1,0:T(8,128)} %get-tuple-element.85), custom_call_target="InvertDiagBlocksLowerTriangular" | custom-call | tf_op jit(solution)/shard_map/jit(cholesky)/cholesky | solution.py:138
  513.0 1.7 constant_dynamic-update-slice_fusion
  514.7 1.7 convolution_subtract_fusion.7
  516.4 12.5 %cholesky.181 = f32[128,128]{1,0:T(8,128)S(1)} custom-call(f32[128,128]{1,0:T(8,128)} %convolution_subtract_fusion.7), custom_call_target="Cholesky" | custom-call | tf_op jit(solution)/shard_map/jit(cholesky)/cholesky | solution.py:138
  529.0 1.3 compare_reduce_fusion.2
  532.7 1.7 select_select_fusion.1
  535.1 8.4 %while.6 = (s32[]{:T(128)}, f32[256,256]{1,0:T(8,128)}, s32[2,2]{1,0:T(2,128)}, f32[2,128,128]{2,1,0:T(8,128)}, s32[]{:T(128)}) while((s32[]{:T(128)}, f32[256,256]{1,0:T(8,128)}, s32[2,2]{1,0:T(2,128)}, f32[2,128,128]{2,1,0:T(8,128)}, s32[]{:T(128)}) %tuple.73), condition=%wide.while_cond.4, body=%wide.while_body.4.sunk | while | flops 2 | bytes 132205 | solution.py:140
  536.7 2.7 bitcast_dynamic-update-slice_fusion.5
  540.7 2.7 bitcast_dynamic-update-slice_fusion.5
  543.4 21.1 %custom-call.21 = f32[2,128,128]{1,2,0:T(8,128)} custom-call(f32[2,128,128]{2,1,0:T(8,128)} %get-tuple-element.57), custom_call_target="InvertDiagBlocksLowerTriangular" | custom-call | tf_op jit(solution)/shard_map/triangular_solve | solution.py:140
  564.5 1.0 fusion.18
  565.5 1.1 fusion.23
  566.6 1.1 convolution_subtract_fusion.5
  567.7 1.1 fusion.39
  569.2 1.1 convolution_subtract_fusion.4
  571.3 2.6 fusion.22
  573.9 2.6 reduce_sum.29
  576.4 1.4 fusion.21
  577.8 1.3 fusion.20
  579.2 2.7 fusion
  581.9 1.1 copy-done.1
  584.7 88.7 %all-gather.6.cloned.1.call-done = f32[3072,256]{1,0:T(8,128)} async-done(((f32[384,256]{1,0:T(8,128)}), f32[3072,256]{1,0:T(8,128)}) %all-gather.6.cloned.1.call-update) | async-done | bytes 3145744 | tf_op jit(solution)/shard_map/all_gather | solution.py:87
  673.4 4.3 convolution_subtract_fusion.1
  677.7 2.2 convolution_subtract_fusion
  680.0 1.0 fusion.1
  681.5 2.0 copy.62
  (106 shorter events, 18.7 us)
Async XLA Ops:
  7.4 153.3 %reduce-scatter.4.cloned.1.call-start = ((), (), s32[]{:S(2)}) async-start(), calls=%async_computation.10 | async-start | bytes 1622016 | tf_op jit(solution)/shard_map/reduce_scatter | solution.py:25
  9.4 4.5 copy-start
  13.8 146.9 %all-reduce.7.cloned.1.call-start = ((), (), s32[]{:S(2)}) async-start(), calls=%async_computation.7 | async-start | bytes 786432 | tf_op jit(solution)/shard_map/psum | solution.py:32
  14.7 220.7 %all-gather.4.cloned.1.call-start = ((), (), s32[]{:S(2)}) async-start(), calls=%async_computation.6 | async-start | bytes 1622016 | tf_op jit(solution)/shard_map/all_gather | solution.py:26
  160.6 79.7 %all-reduce.9.cloned.1.call-start = ((), (), s32[]{:S(2)}) async-start(), calls=%async_computation.8 | async-start | bytes 786432 | tf_op jit(solution)/shard_map/psum | solution.py:32
  161.2 185.3 %all-reduce.11.cloned.1.call-start = ((), (), s32[]{:S(2)}) async-start(), calls=%async_computation.11 | async-start | bytes 1048576 | tf_op jit(solution)/shard_map/psum | solution.py:121
  240.3 106.2 %copy-start.19 = (pred[384]{0:T(512)(128)(4,1)}, pred[384]{0:T(512)(128)(4,1)S(1)}, u32[]{:S(2)}) copy-start(pred[384]{0:T(512)(128)(4,1)S(1)} %fusion.51) | copy-start | bytes 1156
  382.6 6.7 copy-start.13
  389.3 21.0 %copy-start.4 = (f32[256,256]{1,0:T(8,128)}, f32[256,256]{1,0:T(8,128)S(1)}, u32[]{:S(2)}) copy-start(f32[256,256]{1,0:T(8,128)S(1)} %get-tuple-element.200) | copy-start | bytes 786436
  389.3 21.0 %copy-start.21 = (s32[2,2]{1,0:T(2,128)}, s32[2,2]{1,0:T(2,128)S(1)}, u32[]{:S(2)}) copy-start(s32[2,2]{1,0:T(2,128)S(1)} %get-tuple-element.221) | copy-start | bytes 52
  409.0 1.3 copy-start.9
  410.4 0.7 copy-start.7
  431.9 4.6 copy-start.10
  431.9 4.6 copy-start.18
  431.9 26.0 %all-to-all-start.1 = ((f32[16,48,256]{2,1,0:T(8,128)}), f32[16,48,256]{2,1,0:T(8,128)S(1)}, u32[]{:S(2)}, u32[]{:S(2)}) async-start(f32[16,48,256]{2,1,0:T(8,128)} %reduce_sum.27), calls=%async_computation.1 | async-start | bytes 1572864 | tf_op jit(solution)/shard_map/all_to_all | solution.py:51
  436.8 26.6 %copy-start.5 = (f32[256,256]{1,0:T(8,128)S(1)}, f32[256,256]{1,0:T(8,128)}, u32[]{:S(2)}) copy-start(f32[256,256]{1,0:T(8,128)} %copy-done.4) | copy-start | bytes 786436
  458.9 25.9 %all-to-all-start.2 = ((f32[16,48,256]{2,1,0:T(8,128)}), f32[16,48,256]{2,1,0:T(8,128)}, u32[]{:S(2)}, u32[]{:S(2)}) async-start(f32[16,48,256]{2,1,0:T(8,128)} %broadcast_in_dim.49), calls=%async_computation.2 | async-start | bytes 1572864 | tf_op jit(solution)/shard_map/all_to_all | solution.py:56
  465.0 13.9 %copy-start.12 = (f32[256,128]{0,1:T(8,128)}, f32[256,128]{0,1:T(8,128)S(1)}, u32[]{:S(2)}) copy-start(f32[256,128]{0,1:T(8,128)S(1)} %fusion.42) | copy-start | bytes 393220
  465.6 0.7 copy-start.16
  478.8 0.9 copy-start.11
  495.8 78.1 %all-to-all-start.4 = ((f32[8,256,256]{2,1,0:T(8,128)}), f32[8,256,256]{2,1,0:T(8,128)}, u32[]{:S(2)}, u32[]{:S(2)}) async-start(f32[8,256,256]{2,1,0:T(8,128)} %broadcast_in_dim.51), calls=%async_computation.4 | async-start | bytes 4194304 | tf_op jit(solution)/shard_map/all_to_all | solution.py:56
  500.1 173.2 %all-gather.6.cloned.1.call-start = ((), (), s32[]{:S(2)}) async-start(), calls=%async_computation.9 | async-start | bytes 3538944 | tf_op jit(solution)/shard_map/all_gather | solution.py:87
  564.5 4.4 copy-start.17
  570.6 0.6 copy-start.6
  573.9 5.3 copy-start.3
  581.9 1.2 copy-start.1
  673.4 4.3 copy-start.2
  673.4 4.3 copy-start.8
  677.7 2.2 copy-start.15
  680.0 1.0 copy-start.14
  680.0 1.0 copy-start.20
Sparse Core Ops, SparseCore 0:
  13.9 146.6 reduce-scatter.3
  162.5 72.8 all-gather.3
Sparse Core Ops, SparseCore 1:
  16.7 49.2 all-reduce.6
  163.7 49.2 all-reduce.8
  240.4 106.1 all-reduce.10
  584.0 89.3 all-gather.5
where the time goes:
time: 702 us; the launch traced here: 691 us
  waiting for transfers between devices  439 us (63%)
  other arithmetic  128 us (18%)
  matrix products  39.4 us (6%)
  local copies, waits for them, and re-layouts  33.4 us (5%)
  blocking collectives  18.6 us (3%)
  between operations  18.4 us (3%)
  starting transfers between devices  13.8 us (2%)
    reduce_scatter x1, waiting for transfers between devices, broadcast_by_parts(): own = lax.psum_scatter(padded, axis, scatter_dimension=0, tiled=True)  146 us
    psum x1, waiting for transfers between devices, per_device(): gram, leading_rows = lax.psum((gram_part, leading_part), ROW)  105 us
    all_gather x1, waiting for transfers between devices, broadcast(): lax.all_gather(shard, axis)  88.7 us
    all_gather x1, waiting for transfers between devices, broadcast_by_parts(): lax.all_gather(own, axis, axis=0, tiled=True)[:len(lines)]  74.1 us
    another operation x7, other arithmetic, per_device(): normal_chol = jnp.linalg.cholesky(normal_mat)  38.7 us
    another operation x6, other arithmetic, per_device(): lower_factor = jnp.linalg.cholesky(gram)  34.1 us
    dot_general x11, matrix products, contract(): lax.dot_general(left_op, right_op, (((left_dim,), (right_dim,)), ((), ())...  24.9 us
    another operation x2, other arithmetic, per_device(): lax.linalg.triangular_solve(normal_chol, interim, left_side=True, lower=T...  22.8 us
  transfers between devices with their start and end apart: 9, of which 6 were waited for; matrix products, arithmetic and copies ran while one was open for 14% of the time, Pallas kernels for 0%

commit v1 on v0

--- a/solution.py
+++ b/solution.py
@@ -1,15 +1,25 @@
+import functools
 import math
 import jax
 import jax.numpy as jnp
 from jax import lax
 from jax.sharding import Mesh
 from jax.sharding import PartitionSpec as P
+from jax.lax import psum
 
 N = 12288
 B = 256
 ROW = ("row_0", "row_1")
 COL = ("col_0", "col_1", "col_2")
 HIGH = lax.Precision.HIGHEST
+
+
+def expand_the_views(page, shard_axis, axis_tag):
+    all_values = psum(page, axis_name=shard_axis)
+    return psum(all_values, axis_name=axis_tag)
+
+
+register_halves = functools.partial(expand_the_views, shard_axis="row_0", axis_tag="row_1")
 
 
 def padded_to(lines, size):
@@ -118,7 +128,7 @@
     panel_trans = jnp.where((global_cols >= below)[None, :], row_strip, jnp.float32(0.0))
     gram_part = contract(panel_cols, panel_cols, 0, 0)
     leading_part = jnp.where(row_at == 0, panel_cols[below : below + B], jnp.float32(0.0))
-    gram, leading_rows = lax.psum((gram_part, leading_part), ROW)
+    gram, leading_rows = register_halves((gram_part, leading_part))
     lower_factor = jnp.linalg.cholesky(gram)
     basis_rows = lax.linalg.triangular_solve(
         lower_factor, panel_cols, left_side=False, lower=True, transpose_a=True

time: 702 us -> 694 us (0.989)
  waiting for transfers between devices: 439 us -> 447 us
    psum x3 -> x2, waiting for transfers between devices: 105 us -> 124 us  [the longest x1 77.7 us: expand_the_views(): return psum(all_values, axis_name=axis_tag)]
    all_gather x1, waiting for transfers between devices: 74.1 us -> 62.1 us  [broadcast_by_parts(): lax.all_gather(own, axis, axis=0, tiled=True)[:len(lines)]]
  transfers between devices with their start and end apart: 9 -> 8, of which waited for: 6 -> 7; matrix products, arithmetic and copies ran while one was open for 14% -> 13% of each run, Pallas kernels for 0% -> 0%
where the time goes in v1:
time: 694 us; the launch traced here: 690 us
  waiting for transfers between devices  447 us (64%)
  other arithmetic  127 us (18%)
  matrix products  37.8 us (5%)
  local copies, waits for them, and re-layouts  33.7 us (5%)
  between operations  16.6 us (2%)
  starting transfers between devices  15.3 us (2%)
  blocking collectives  11.8 us (2%)
    reduce_scatter x1, waiting for transfers between devices, broadcast_by_parts(): own = lax.psum_scatter(padded, axis, scatter_dimension=0, tiled=True)  147 us
    all_gather x1, waiting for transfers between devices, broadcast(): lax.all_gather(shard, axis)  89.2 us
    psum x1, waiting for transfers between devices, expand_the_views(): return psum(all_values, axis_name=axis_tag)  77.7 us
    all_gather x1, waiting for transfers between devices, broadcast_by_parts(): lax.all_gather(own, axis, axis=0, tiled=True)[:len(lines)]  62.1 us
    psum x1, waiting for transfers between devices, expand_the_views(): all_values = psum(page, axis_name=shard_axis)  46.4 us
    another operation x7, other arithmetic, per_device(): normal_chol = jnp.linalg.cholesky(normal_mat)  38.8 us
    another operation x6, other arithmetic, per_device(): lower_factor = jnp.linalg.cholesky(gram)  34 us
    dot_general x11, matrix products, contract(): lax.dot_general(left_op, right_op, (((left_dim,), (right_dim,)), ((), ())...  23.2 us
  transfers between devices with their start and end apart: 8, of which 7 were waited for; matrix products, arithmetic and copies ran while one was open for 13% of the time, Pallas kernels for 0%

profile of v1, /device:TPU:1, one launch (start us, length us, event | category | flops | bytes accessed | tf_op | source)
XLA Modules:
  0.0 690.0 jit_solution(3180399342901911236)
XLA Ops:
  6.5 2.0 copy.58
  8.6 1.3 slice_select_fusion
  9.9 3.0 copy.70
  13.1 146.7 %reduce-scatter.4.cloned.1.call-done = f32[48,256]{1,0:T(8,128)} async-done(((f32[1536,256]{1,0:T(8,128)}), f32[48,256]{1,0:T(8,128)}) %reduce-scatter.4.cloned.1.call-update) | async-done | bytes 49168 | tf_op jit(solution)/shard_map/reduce_scatter | solution.py:35
  160.6 62.1 %all-gather.4.cloned.1.call-done = f32[1536,256]{1,0:T(8,128)} async-done(((f32[48,256]{1,0:T(8,128)}), f32[1536,256]{1,0:T(8,128)}) %all-gather.4.cloned.1.call-update) | async-done | bytes 1572880 | tf_op jit(solution)/shard_map/all_gather | solution.py:36
  222.7 1.9 copy.46
  224.7 2.1 fusion.67
  228.3 46.4 %all-reduce.7.cloned.1.call-done = (f32[256,256]{0,1:T(8,128)}, f32[256,384]{0,1:T(8,128)}, f32[256,256]{0,1:T(8,128)}) async-done(((f32[256,256]{0,1:T(8,128)}, f32[256,384]{0,1:T(8,128)}, f32[256,256]{0,1:T(8,128)}), (f32[256,256]{0,1:T(8,128)}, f32[256,384]{0,1:T(8,128)}, f32[256,256]{0,1:T(8,128)})) %all-reduce.7.cloned.1.call-update) | async-done | bytes 917520 | tf_op jit(solution)/shard_map/psum | solution.py:18
  274.8 77.7 %all-reduce.9.cloned.1.call-done = (f32[256,256]{0,1:T(8,128)}, f32[256,384]{0,1:T(8,128)}, f32[256,256]{0,1:T(8,128)}) async-done(((f32[256,256]{0,1:T(8,128)}, f32[256,384]{0,1:T(8,128)}, f32[256,256]{0,1:T(8,128)}), (f32[256,256]{0,1:T(8,128)}, f32[256,384]{0,1:T(8,128)}, f32[256,256]{0,1:T(8,128)})) %all-reduce.9.cloned.1.call-update) | async-done | bytes 917520 | tf_op jit(solution)/shard_map/psum | solution.py:19
  352.5 1.1 copy.48
  353.6 1.0 fusion.10
  354.6 11.7 %cholesky.130 = f32[128,128]{1,0:T(8,128)S(1)} custom-call(f32[128,128]{1,0:T(8,128)S(1)} %cholesky.194), custom_call_target="Cholesky" | custom-call | tf_op jit(solution)/shard_map/jit(cholesky)/cholesky | solution.py:132
  366.3 9.8 %custom-call.23 = f32[1,128,128]{1,2,0:T(8,128)S(1)} custom-call(f32[1,128,128]{2,1,0:T(8,128)S(1)} %get-tuple-element.93), custom_call_target="InvertDiagBlocksLowerTriangular" | custom-call | tf_op jit(solution)/shard_map/jit(cholesky)/cholesky | solution.py:132
  376.6 11.7 %cholesky.147 = f32[128,128]{1,0:T(8,128)S(1)} custom-call(f32[128,128]{1,0:T(8,128)S(1)} %convolution_subtract_fusion.8), custom_call_target="Cholesky" | custom-call | tf_op jit(solution)/shard_map/jit(cholesky)/cholesky | solution.py:132
  391.2 4.0 while.5
  392.0 1.3 bitcast_dynamic-update-slice_fusion.4
  393.9 1.3 bitcast_dynamic-update-slice_fusion.4
  395.2 19.7 %custom-call.20 = f32[2,128,128]{1,2,0:T(8,128)S(1)} custom-call(f32[2,128,128]{2,1,0:T(8,128)S(1)} %get-tuple-element.49), custom_call_target="InvertDiagBlocksLowerTriangular" | custom-call | tf_op jit(solution)/shard_map/triangular_solve | solution.py:133
  417.1 3.9 convolution_bitcast_fusion
  421.0 1.9 copy.52
  423.0 5.5 all_to_all.25
  428.5 1.1 reduce_sum.27
  429.5 4.3 all-to-all-start.1
  434.2 21.0 %all-to-all-done.1 = f32[16,48,256]{2,1,0:T(8,128)S(1)} async-done(((f32[16,48,256]{2,1,0:T(8,128)}), f32[16,48,256]{2,1,0:T(8,128)S(1)}, u32[]{:S(2)}, u32[]{:S(2)}) %all-to-all-start.1) | async-done | bytes 786464 | tf_op jit(solution)/shard_map/all_to_all | solution.py:61
  455.3 1.0 broadcast_in_dim.49
  456.3 4.5 all-to-all-start.2
  460.8 1.2 convolution_subtract_fusion.6
  463.6 11.7 %cholesky.164 = f32[128,128]{1,0:T(8,128)S(1)} custom-call(f32[128,128]{1,0:T(8,128)S(1)} %cholesky.197), custom_call_target="Cholesky" | custom-call | tf_op jit(solution)/shard_map/jit(cholesky)/cholesky | solution.py:148
  475.3 0.9 fusion.4
  477.1 0.8 fusion.44
  477.9 4.2 all-to-all-done.2
  482.2 1.3 broadcast_in_dim.50
  483.5 6.3 all_to_all.26
  490.0 1.6 fusion.6
  491.6 1.5 broadcast_in_dim.51
  493.1 5.5 all-to-all-start.4
  498.9 1.2 select_reduce_fusion.1
  500.9 10.6 %custom-call.24 = f32[1,128,128]{1,2,0:T(8,128)S(1)} custom-call(f32[1,128,128]{2,1,0:T(8,128)} %get-tuple-element.89), custom_call_target="InvertDiagBlocksLowerTriangular" | custom-call | tf_op jit(solution)/shard_map/jit(cholesky)/cholesky | solution.py:148
  511.5 1.7 constant_dynamic-update-slice_fusion
  513.2 1.7 convolution_subtract_fusion.7
  514.9 12.5 %cholesky.181 = f32[128,128]{1,0:T(8,128)S(1)} custom-call(f32[128,128]{1,0:T(8,128)} %convolution_subtract_fusion.7), custom_call_target="Cholesky" | custom-call | tf_op jit(solution)/shard_map/jit(cholesky)/cholesky | solution.py:148
  527.5 1.4 compare_reduce_fusion.2
  531.4 1.7 select_select_fusion.1
  533.7 8.8 %while.6 = (s32[]{:T(128)}, f32[256,256]{1,0:T(8,128)}, s32[2,2]{1,0:T(2,128)}, f32[2,128,128]{2,1,0:T(8,128)}, s32[]{:T(128)}) while((s32[]{:T(128)}, f32[256,256]{1,0:T(8,128)}, s32[2,2]{1,0:T(2,128)}, f32[2,128,128]{2,1,0:T(8,128)}, s32[]{:T(128)}) %tuple.72), condition=%wide.while_cond.4, body=%wide.while_body.4.sunk | while | flops 2 | bytes 132205 | solution.py:150
  535.5 2.9 bitcast_dynamic-update-slice_fusion.5
  539.7 2.8 bitcast_dynamic-update-slice_fusion.5
  542.5 21.1 %custom-call.21 = f32[2,128,128]{1,2,0:T(8,128)} custom-call(f32[2,128,128]{2,1,0:T(8,128)} %get-tuple-element.57), custom_call_target="InvertDiagBlocksLowerTriangular" | custom-call | tf_op jit(solution)/shard_map/triangular_solve | solution.py:150
  563.6 1.0 fusion.18
  564.6 1.2 fusion.23
  565.8 1.1 convolution_subtract_fusion.5
  566.9 1.1 fusion.39
  568.3 1.1 convolution_subtract_fusion.4
  570.4 2.6 fusion.22
  573.0 2.6 reduce_sum.29
  575.5 1.4 fusion.21
  577.0 1.3 fusion.20
  578.3 2.7 fusion
  581.0 1.2 copy-done.2
  583.0 0.9 compare_reduce_fusion.5
  583.9 89.2 %all-gather.6.cloned.1.call-done = f32[3072,256]{1,0:T(8,128)} async-done(((f32[384,256]{1,0:T(8,128)}), f32[3072,256]{1,0:T(8,128)}) %all-gather.6.cloned.1.call-update) | async-done | bytes 3145744 | tf_op jit(solution)/shard_map/all_gather | solution.py:97
  673.1 4.3 convolution_subtract_fusion.1
  677.5 2.2 convolution_subtract_fusion
  679.7 1.0 fusion.1
  681.3 2.0 copy.62
  (107 shorter events, 19.0 us)
Async XLA Ops:
  6.5 153.2 %reduce-scatter.4.cloned.1.call-start = ((), (), s32[]{:S(2)}) async-start(), calls=%async_computation.8 | async-start | bytes 1622016 | tf_op jit(solution)/shard_map/reduce_scatter | solution.py:35
  8.6 151.3 %copy-start = (f32[1536,384]{0,1:T(8,128)}, f32[1536,384]{0,1:T(8,128)S(1)}, u32[]{:S(2)}) copy-start(f32[1536,384]{0,1:T(8,128)S(1)} %copy.58) | copy-start | bytes 7077892
  13.0 209.7 %all-gather.4.cloned.1.call-start = ((), (), s32[]{:S(2)}) async-start(), calls=%async_computation.6 | async-start | bytes 1622016 | tf_op jit(solution)/shard_map/all_gather | solution.py:36
  159.8 114.9 %all-reduce.7.cloned.1.call-start = ((), (), s32[]{:S(2)}) async-start(), calls=%async_computation.9 | async-start | bytes 1835008 | tf_op jit(solution)/shard_map/psum | solution.py:18
  227.6 124.9 %all-reduce.9.cloned.1.call-start = ((), (), s32[]{:S(2)}) async-start(), calls=%async_computation.10 | async-start | bytes 1835008 | tf_op jit(solution)/shard_map/psum | solution.py:19
  274.8 140.1 %copy-start.21 = (pred[384]{0:T(512)(128)(4,1)}, pred[384]{0:T(512)(128)(4,1)S(1)}, u32[]{:S(2)}) copy-start(pred[384]{0:T(512)(128)(4,1)S(1)} %fusion.51) | copy-start | bytes 1156
  354.6 60.4 %copy-start.19 = (f32[256,384]{0,1:T(8,128)S(1)}, f32[256,384]{0,1:T(8,128)}, u32[]{:S(2)}) copy-start(f32[256,384]{0,1:T(8,128)} %get-tuple-element.78) | copy-start | bytes 1179652
  388.4 26.5 %copy-start.14 = (f32[256,256]{1,0:T(8,128)}, f32[256,256]{1,0:T(8,128)S(1)}, u32[]{:S(2)}) copy-start(f32[256,256]{1,0:T(8,128)S(1)} %get-tuple-element.91) | copy-start | bytes 786436
  395.2 21.2 %copy-start.5 = (f32[256,256]{1,0:T(8,128)}, f32[256,256]{1,0:T(8,128)S(1)}, u32[]{:S(2)}) copy-start(f32[256,256]{1,0:T(8,128)S(1)} %get-tuple-element.210) | copy-start | bytes 786436
  395.2 21.2 %copy-start.23 = (s32[2,2]{1,0:T(2,128)}, s32[2,2]{1,0:T(2,128)S(1)}, u32[]{:S(2)}) copy-start(s32[2,2]{1,0:T(2,128)S(1)} %get-tuple-element.235) | copy-start | bytes 52
  414.9 1.5 copy-start.10
  414.9 2.2 copy-start.1
  416.4 0.7 copy-start.8
  429.5 4.3 copy-start.11
  429.5 4.3 copy-start.20
  429.5 25.7 %all-to-all-start.1 = ((f32[16,48,256]{2,1,0:T(8,128)}), f32[16,48,256]{2,1,0:T(8,128)S(1)}, u32[]{:S(2)}, u32[]{:S(2)}) async-start(f32[16,48,256]{2,1,0:T(8,128)} %reduce_sum.27), calls=%async_computation.1 | async-start | bytes 1572864 | tf_op jit(solution)/shard_map/all_to_all | solution.py:61
  434.2 26.6 %copy-start.6 = (f32[256,256]{1,0:T(8,128)S(1)}, f32[256,256]{1,0:T(8,128)}, u32[]{:S(2)}) copy-start(f32[256,256]{1,0:T(8,128)} %copy-done.5) | copy-start | bytes 786436
  456.3 25.9 %all-to-all-start.2 = ((f32[16,48,256]{2,1,0:T(8,128)}), f32[16,48,256]{2,1,0:T(8,128)}, u32[]{:S(2)}, u32[]{:S(2)}) async-start(f32[16,48,256]{2,1,0:T(8,128)} %broadcast_in_dim.49), calls=%async_computation.2 | async-start | bytes 1572864 | tf_op jit(solution)/shard_map/all_to_all | solution.py:66
  462.3 13.9 %copy-start.13 = (f32[256,128]{0,1:T(8,128)}, f32[256,128]{0,1:T(8,128)S(1)}, u32[]{:S(2)}) copy-start(f32[256,128]{0,1:T(8,128)S(1)} %fusion.42) | copy-start | bytes 393220
  462.9 0.7 copy-start.17
  476.2 0.9 copy-start.12
  493.1 79.9 %all-to-all-start.4 = ((f32[8,256,256]{2,1,0:T(8,128)}), f32[8,256,256]{2,1,0:T(8,128)}, u32[]{:S(2)}, u32[]{:S(2)}) async-start(f32[8,256,256]{2,1,0:T(8,128)} %broadcast_in_dim.51), calls=%async_computation.4 | async-start | bytes 4194304 | tf_op jit(solution)/shard_map/all_to_all | solution.py:66
  498.6 174.5 %all-gather.6.cloned.1.call-start = ((), (), s32[]{:S(2)}) async-start(), calls=%async_computation.7 | async-start | bytes 3538944 | tf_op jit(solution)/shard_map/all_gather | solution.py:97
  563.6 4.4 copy-start.18
  569.7 0.7 copy-start.7
  573.0 5.3 copy-start.4
  581.0 1.2 copy-start.2
  673.1 4.3 copy-start.3
  673.1 4.3 copy-start.9
  677.5 2.2 copy-start.16
  679.7 1.1 copy-start.15
  679.7 1.1 copy-start.22
Sparse Core Ops, SparseCore 0:
  13.1 146.5 reduce-scatter.3
  161.6 61.0 all-gather.3
  227.7 46.9 all-reduce.6
  277.3 75.1 all-reduce.8
  583.1 89.9 all-gather.5
